TPU v7x, 512 devices: a whole 4x8x8 slice. The times are simulated.
512 devices in a mesh: grp: 8 (over z), row: 64 (over y, x, core).
Axes of the slice: x: 4, y: 8, z: 8, core: 2. Of those that a mesh axis runs over, the one named last changes fastest.
Arguments:
- tiles: bfloat16 [3072, 512, 512], P(('grp', 'row')), may hold values from -0.15625 to 0.15625
- tile_row: int32 [3072], P(('grp', 'row')), may hold values from 0 to 1023, as said below
- tile_col: int32 [3072], P(('grp', 'row')), may hold values from 0 to 1023, as said below
- tile_count: int32 [512], P(('grp', 'row')), may hold values from 3 to 6, as said below
- q_block: bfloat16 [524288, 256], P(('grp', 'row')), may hold values from -80 to 80
Outputs:
- q_next: float32 [524288, 256], P(('grp', 'row'))
Inputs may be any that keep to these rules, and one draw needn't show every extreme that they name: `tile_row`: each slot names one of its device's tile rows: d * 2 to d * 2 + 1 for device d. `tile_col`: each slot's tile column is (tile_row + o) mod 1024 with o from minus 2 to 2; no two slots of one device name the same pair of tile row and tile column. `tile_count`: some device has all 6 slots live.
All inputs are finite; a program needn't handle non-finite values.
Results may differ from a plain program's by a relative error of at most 0.0029.
Values may be sent and summed in bfloat16 or wider, within the bound.
A program may use at most 64 MiB of HBM per device.

v0:
```python
import jax
import jax.numpy as jnp
from jax import lax
from jax.sharding import Mesh
from jax.sharding import PartitionSpec as P

H = 2
ROW = ("row_0", "row_1", "row_2")
GRP_ROW = ("grp", "row_0", "row_1", "row_2")


def with_halo(x, sides, width):
    edges = {}
    for axis, dim in sides:
        peers, length = (lax.axis_size(axis), x.shape[dim])
        up = [(i, (i + 1) % peers) for i in range(peers)]
        last = lax.slice_in_dim(x, length - width, length, axis=dim)
        initial = lax.slice_in_dim(x, 0, width, axis=dim)
        edges[dim] = (
            lax.ppermute(last, axis, up),
            lax.ppermute(initial, axis, [(b, a) for a, b in up]),
        )
    done = []
    for _, dim in sides:
        low, high = edges[dim]
        around = [(width, width) if d in done else (0, 0) for d in range(x.ndim)]
        x = jnp.concatenate([jnp.pad(low, around), x, jnp.pad(high, around)], axis=dim)
        done.append(dim)
    return x


def split_up(x, dim, peers):
    lengths = x.shape
    tiles = x.reshape(*lengths[:dim], peers, lengths[dim] // peers, *lengths[dim + 1 :])
    return jnp.moveaxis(tiles, dim, 0)


def summed_on_arrival(x, axis, dim):
    tiles = split_up(x, dim, lax.axis_size(axis))
    arrived = lax.all_to_all(tiles, axis, split_axis=0, concat_axis=0, tiled=True)
    return arrived.astype(jnp.float32).sum(axis=0)


def sum_in_two_steps(x, axes, dim):
    far, near = axes
    own = summed_on_arrival(split_up(x, dim, lax.axis_size(far)), near, dim + 1)
    return jnp.sum(
        lax.all_to_all(own.astype(jnp.bfloat16), far, 0, 0, tiled=True).astype(jnp.float32), axis=0
    )


def padded_to(lines, peers):
    spare = -len(lines) % peers
    return jnp.pad(lines, [(0, spare)] + [(0, 0)] * (lines.ndim - 1))


def from_everyone(x, axis):
    copies = jnp.broadcast_to(x, (lax.axis_size(axis), *x.shape))
    return lax.all_to_all(copies, axis, split_axis=0, concat_axis=0, tiled=True)


def in_order(tiles, dim):
    tiles = jnp.moveaxis(tiles, 0, dim)
    lengths = tiles.shape
    return tiles.reshape(*lengths[:dim], lengths[dim] * lengths[dim + 1], *lengths[dim + 2 :])


def gathered_by_axis(x, axes, dim):
    far, near = axes
    tiles = from_everyone(from_everyone(x, far), near)
    return in_order(tiles.swapaxes(0, 1).reshape(-1, *x.shape), dim)


def nested_sum(x, axes):
    lines = x.reshape(-1)
    own = sum_in_two_steps(
        padded_to(lines, lax.axis_size(axes[0]) * lax.axis_size(axes[1])), axes, 0
    )
    whole = gathered_by_axis(own.astype(jnp.bfloat16), axes, 0)
    return whole[: len(lines)].reshape(x.shape).astype(jnp.float32)


def on_device(tiles, tile_row, tile_col, tile_count, q_block):
    slot_count, tile_size, unused_size = tiles.shape
    basis_width = q_block.shape[1]
    own_tiles = q_block.shape[0] // tile_size
    window = own_tiles + 2 * H
    tile_total = own_tiles * lax.axis_size("grp") * lax.axis_size(ROW)
    local_row = tile_row % own_tiles
    local_col = (tile_col - tile_row + H) % tile_total + local_row
    padded = with_halo(q_block, ((GRP_ROW, 0),), H * tile_size)
    stack = padded.reshape(window, tile_size, basis_width)
    live_slot = jnp.arange(slot_count, dtype=jnp.int32) < tile_count[0]
    blocks = stack[local_col]
    blocks = jnp.where(live_slot[:, None, None], blocks, jnp.zeros_like(blocks))
    products = jnp.einsum("sab,sbk->sak", tiles, blocks, preferred_element_type=jnp.float32)
    row_ids = jnp.arange(own_tiles, dtype=jnp.int32)
    row_place = ((local_row[None, :] == row_ids[:, None]) & live_slot[None, :]).astype(jnp.float32)
    aq_tiles = jnp.einsum(
        "rs,sak->rak", row_place, products, precision=lax.Precision.HIGHEST
    ).astype(jnp.bfloat16)
    row_part = aq_tiles[local_row]
    images = jnp.einsum("sab,sak->sbk", tiles, row_part, preferred_element_type=jnp.float32)
    column_ids = jnp.arange(window, dtype=jnp.int32)
    col_place = ((local_col[None, :] == column_ids[:, None]) & live_slot[None, :]).astype(
        jnp.float32
    )
    sums = jnp.einsum("cs,sbk->cbk", col_place, images, precision=lax.Precision.HIGHEST)
    own_part = sums[H : H + own_tiles]
    lower = sums[:H].astype(jnp.bfloat16).reshape(H * tile_size, basis_width)
    upper = sums[H + own_tiles :].astype(jnp.bfloat16).reshape(H * tile_size, basis_width)
    edges = with_halo(jnp.concatenate([lower, upper], axis=0), ((GRP_ROW, 0),), H * tile_size)
    from_below = edges[: H * tile_size]
    from_above = edges[edges.shape[0] - H * tile_size :]
    below_tiles = from_below.astype(jnp.float32).reshape(H, tile_size, basis_width)
    above_tiles = from_above.astype(jnp.float32).reshape(H, tile_size, basis_width)
    own_part = own_part + below_tiles
    own_part = own_part + above_tiles
    local_y = own_part.reshape(own_tiles * tile_size, basis_width)
    rows_total = tile_total * tile_size
    local_gram = jnp.dot(
        local_y.T, local_y, precision=lax.Precision.HIGHEST, preferred_element_type=jnp.float32
    )
    gram_matrix = (
        nested_sum(local_gram.astype(jnp.bfloat16), (("grp", "row_0"), ("row_1", "row_2")))
        / rows_total
    )
    factor_low = jnp.linalg.cholesky(gram_matrix)
    return lax.linalg.triangular_solve(
        factor_low, local_y, left_side=False, lower=True, transpose_a=True
    )


def solution(mesh):
    torus = Mesh(
        mesh.devices.reshape(mesh.shape["grp"], 8, 4, 2), ("grp", "row_0", "row_1", "row_2")
    )
    return jax.shard_map(
        on_device,
        mesh=torus,
        in_specs=(P(GRP_ROW, None, None), P(GRP_ROW), P(GRP_ROW), P(GRP_ROW), P(GRP_ROW, None)),
        out_specs=P(GRP_ROW, None),
        check_vma=False,
    )
```

profile of v0, /device:TPU:1, one launch (start us, length us, event | category | flops | bytes accessed | tf_op | source)
XLA Modules:
  0.0 215.5 jit_solution(11528828650594353785)
XLA Ops:
  0.0 0.0 copy-start
  0.0 4.8 %collective-permute-start = (bf16[1024,256]{1,0:T(8,128)(2,1)}, bf16[1024,256]{1,0:T(8,128)(2,1)S(1)}, u32[]{:S(2)}, u32[]{:S(2)}) collective-permute-start(bf16[1024,256]{1,0:T(8,128)(2,1)} %param.9), channel_id=1, source_target_pairs={{0,1},{1,2},{2,3},{3,4},{4,5},{5,6},{6,7},{7,8},{8,9},{9,10},{10,1... | collective-permute-start | bytes 1572872 | tf_op jit(solution)/shard_map/ppermute | solution.py:20
  4.8 6.2 %collective-permute-start.1 = (bf16[1024,256]{1,0:T(8,128)(2,1)}, bf16[1024,256]{1,0:T(8,128)(2,1)S(1)}, u32[]{:S(2)}, u32[]{:S(2)}) collective-permute-start(bf16[1024,256]{1,0:T(8,128)(2,1)} %param.9), channel_id=1, source_target_pairs={{1,0},{2,1},{3,2},{4,3},{5,4},{6,5},{7,6},{8,7},{9,8},{10,9},{11,1... | collective-permute-start | bytes 1572872 | tf_op jit(solution)/shard_map/ppermute | solution.py:21
  10.9 0.7 compare_select_fusion
  12.3 0.7 compare_select_fusion.1
  13.0 0.0 collective-permute-done
  13.0 2.5 %collective-permute-done.1 = bf16[1024,256]{1,0:T(8,128)(2,1)S(1)} collective-permute-done((bf16[1024,256]{1,0:T(8,128)(2,1)}, bf16[1024,256]{1,0:T(8,128)(2,1)S(1)}, u32[]{:S(2)}, u32[]{:S(2)}) %collective-permute-start.1) | collective-permute-done | bytes 524320 | tf_op jit(solution)/shard_map/ppermute | solution.py:21
  15.5 2.3 %pad_maximum_fusion = bf16[3072,256]{1,0:T(8,128)(2,1)} fusion(bf16[1024,256]{1,0:T(8,128)(2,1)S(1)} %collective-permute-done.1, bf16[1024,256]{1,0:T(8,128)(2,1)} %param.9, bf16[1024,256]{1,0:T(8,128)(2,1)S(1)} %collective-permute-done), kind=kLoop, calls=%fused_computation.6 | loop fusion | flops 4718592 | bytes 3145728 | tf_op jit(solution)/shard_map/concatenate | solution.py:27
  17.8 3.3 %gather_fusion = bf16[6,512,256]{2,1,0:T(8,128)(2,1)} fusion(bf16[6,512,256]{2,1,0:T(8,128)(2,1)} %bitcast.74, s32[1024]{0:T(1024)S(1)} %pad_clamp_fusion.1), kind=kCustom, calls=%fused_computation | custom fusion | bytes 3145752 | tf_op jit(solution)/shard_map/gather | solution.py:94
  21.1 0.0 copy-done
  21.1 4.3 %convolution_bitcast_fusion.1 = f32[6,512,256]{1,2,0:T(8,128)} fusion(bf16[6,512,512]{2,1,0:T(8,128)(2,1)S(1)} %copy-done, bf16[6,512,256]{2,1,0:T(8,128)(2,1)} %gather_fusion, pred[6]{0:T(512)(128)(4,1)S(1)} %iota_compare_fusion.4), kind=kOutput, calls=%fused_computation.5 | convolution fusion | flops 806092800 | bytes 7864326 | tf_op jit(solution)/shard_map/sab,sbk->sak/dot_general | solution.py:96
  25.3 5.1 %copy.51 = f32[6,512,256]{2,0,1:T(8,128)} copy(f32[6,512,256]{1,2,0:T(8,128)} %convolution_bitcast_fusion.1) | data formatting | bytes 6291456 | tf_op jit(solution)/shard_map/sab,sbk->sak/dot_general | solution.py:96
  30.4 4.3 %convolution_convert_fusion = bf16[2,512,256]{2,0,1:T(2,128)(2,1)S(1)} fusion(f32[6,512,256]{2,0,1:T(8,128)} %copy.51, pred[6]{0:T(512)(128)(4,1)S(1)} %iota_compare_fusion.4, s32[6]{0:T(128)S(1)} %get-tuple-element.22), kind=kOutput, calls=%fused_computation.9 | convolution fusion | flops 19136536 | bytes 3670046 | tf_op jit(solution)/shard_map/rs,sak->rak/dot_general | solution.py:99
  34.7 0.9 copy.52
  35.6 2.9 %gather_fusion.1 = bf16[6,512,256]{2,1,0:T(8,128)(2,1)} fusion(bf16[2,512,256]{2,1,0:T(8,128)(2,1)} %copy.52, s32[1024]{0:T(1024)S(1)} %pad_clamp_fusion), kind=kCustom, calls=%fused_computation.1 | custom fusion | bytes 3145752 | tf_op jit(solution)/shard_map/gather | solution.py:102
  38.5 4.1 %convolution_bitcast_fusion = f32[6,512,256]{1,2,0:T(8,128)} fusion(bf16[6,512,256]{2,1,0:T(8,128)(2,1)} %gather_fusion.1, bf16[6,512,512]{2,1,0:T(8,128)(2,1)S(1)} %copy-done), kind=kOutput, calls=%fused_computation.4 | convolution fusion | flops 805306368 | bytes 7864320 | tf_op jit(solution)/shard_map/sab,sak->sbk/dot_general | solution.py:103
  42.6 5.1 %copy.54 = f32[6,512,256]{2,0,1:T(8,128)} copy(f32[6,512,256]{1,2,0:T(8,128)} %convolution_bitcast_fusion) | data formatting | bytes 6291456 | tf_op jit(solution)/shard_map/sab,sak->sbk/dot_general | solution.py:103
  47.7 4.3 %fusion.33 = (bf16[6,512,256]{2,0,1:T(8,128)(2,1)S(1)}, f32[6,512,256]{2,0,1:T(8,128)S(1)}) fusion(f32[6,512,256]{2,0,1:T(8,128)} %copy.54, s32[6]{0:T(128)S(1)} %get-tuple-element.24, pred[6]{0:T(512)(128)(4,1)S(1)} %iota_compare_fusion.4), kind=kOutput, calls=%fused_computation.74 | convolution fusion | flops 57409608 | bytes 7864350 | tf_op jit(solution)/shard_map/cs,sbk->cbk/dot_general | solution.py:108
  52.0 0.7 fusion.32
  52.7 0.1 copy.56
  52.8 1.9 collective-permute-start.2
  54.8 0.1 copy.57
  54.8 12.6 %collective-permute-start.3 = (bf16[1024,256]{1,0:T(8,128)(2,1)S(1)}, bf16[1024,256]{1,0:T(8,128)(2,1)S(1)}, u32[]{:S(2)}, u32[]{:S(2)}) collective-permute-start(bf16[1024,256]{1,0:T(8,128)(2,1)S(1)} %bitcast.76), channel_id=1, source_target_pairs={{1,0},{2,1},{3,2},{4,3},{5,4},{6,5},{7,6},{8,7},{9,8},{10,9},{11,1... | collective-permute-start | bytes 1572872 | tf_op jit(solution)/shard_map/ppermute | solution.py:21
  67.4 0.5 slice.71
  68.0 0.0 collective-permute-done.2
  68.0 1.0 collective-permute-done.3
  69.0 0.1 fusion.3
  69.1 0.0 copy-start.1
  69.1 1.0 copy-done.1
  70.1 1.8 fusion.2
  72.0 20.2 %all_to_all.28 = bf16[8,64,128]{2,1,0:T(8,128)(2,1)S(1)} all-to-all(bf16[8,64,128]{2,1,0:T(8,128)(2,1)S(1)} %bitcast.77), channel_id=1, replica_groups=mesh['grp'=8,'row_0'=8,'row_1'=4,'row_2'=2] {'row_1','row_2'}, dimensions={0} | all-to-all | bytes 262144 | tf_op jit(solution)/shard_map/all_to_all | solution.py:40
  92.3 19.1 %all_to_all.29 = bf16[64,1,128]{2,1,0:T(2,128)(2,1)S(1)} all-to-all(bf16[64,1,128]{2,1,0:T(2,128)(2,1)S(1)} %copy.60), channel_id=1, replica_groups=mesh['grp'=8,'row_0'=8,'row_1'=4,'row_2'=2] {'grp','row_0'}, dimensions={0} | all-to-all | bytes 32768 | tf_op jit(solution)/shard_map/all_to_all | solution.py:48
  111.3 0.1 reduce_sum.25
  111.5 14.7 %all_to_all.30 = bf16[64,1,128]{2,1,0:T(2,128)(2,1)S(1)} all-to-all(bf16[64,1,128]{2,1,0:T(2,128)(2,1)S(1)} %broadcast_in_dim.36), channel_id=1, replica_groups=mesh['grp'=8,'row_0'=8,'row_1'=4,'row_2'=2] {'grp','row_0'}, dimensions={0} | all-to-all | bytes 32768 | tf_op jit(solution)/shard_map/all_to_all | solution.py:59
  126.1 0.7 broadcast_in_dim.37
  126.8 6.7 %all-to-all-start.3 = ((bf16[8,64,128]{2,1,0:T(8,128)(2,1)}), bf16[8,64,128]{2,1,0:T(8,128)(2,1)S(1)}, u32[]{:S(2)}, u32[]{:S(2)}) async-start(bf16[8,64,128]{2,1,0:T(8,128)(2,1)} %broadcast_in_dim.37), calls=%async_computation.3 | async-start | bytes 262144 | tf_op jit(solution)/shard_map/all_to_all | solution.py:59
  133.5 5.3 %all-to-all-done.3 = bf16[8,64,128]{2,1,0:T(8,128)(2,1)S(1)} async-done(((bf16[8,64,128]{2,1,0:T(8,128)(2,1)}), bf16[8,64,128]{2,1,0:T(8,128)(2,1)S(1)}, u32[]{:S(2)}, u32[]{:S(2)}) %all-to-all-start.3) | async-done | bytes 131104 | tf_op jit(solution)/shard_map/all_to_all | solution.py:59
  138.8 0.8 copy.61
  139.6 1.0 div.21
  140.7 0.8 copy.62
  141.5 1.0 fusion.8
  142.5 0.0 copy-start.3
  142.5 0.7 copy-done.3
  143.2 11.7 %cholesky.50 = f32[128,128]{1,0:T(8,128)S(1)} custom-call(f32[128,128]{1,0:T(8,128)S(1)} %cholesky.118), custom_call_target="Cholesky" | custom-call | tf_op jit(solution)/shard_map/jit(cholesky)/cholesky | solution.py:128
  154.9 9.8 %custom-call.14 = f32[1,128,128]{1,2,0:T(8,128)S(1)} custom-call(f32[1,128,128]{2,1,0:T(8,128)S(1)} %get-tuple-element.32), custom_call_target="InvertDiagBlocksLowerTriangular" | custom-call | tf_op jit(solution)/shard_map/jit(cholesky)/cholesky | solution.py:128
  164.8 1.0 constant_dynamic-update-slice_fusion.1
  165.8 1.1 convolution_subtract_fusion
  166.9 11.7 %cholesky.105 = f32[128,128]{1,0:T(8,128)S(1)} custom-call(f32[128,128]{1,0:T(8,128)S(1)} %convolution_subtract_fusion), custom_call_target="Cholesky" | custom-call | tf_op jit(solution)/shard_map/jit(cholesky)/cholesky | solution.py:128
  178.7 0.0 copy-start.2
  178.7 0.7 compare_reduce_fusion
  180.8 0.0 copy-done.2
  180.8 1.0 select_select_fusion
  181.8 0.1 triangular_solve.58
  181.8 5.2 %while.1 = (s32[]{:T(128)}, f32[256,256]{1,0:T(8,128)S(1)}, s32[2,2]{1,0:T(2,128)S(1)}, f32[2,128,128]{2,1,0:T(8,128)}, s32[]{:T(128)}) while((s32[]{:T(128)}, f32[256,256]{1,0:T(8,128)S(1)}, s32[2,2]{1,0:T(2,128)S(1)}, f32[2,128,128]{2,1,0:T(8,128)}, s32[]{:T(128)}) %tuple.27), condition=%wide.while_cond, body=%wide.while_body.sunk | while | flops 2 | bytes 132705 | solution.py:129
  181.8 0.6 fusion.45
  182.5 2.0 bitcast_dynamic-update-slice_fusion.2
  184.5 0.6 fusion.45
  185.1 2.0 bitcast_dynamic-update-slice_fusion.2
  187.1 20.5 %custom-call.15 = f32[2,128,128]{1,2,0:T(8,128)S(1)} custom-call(f32[2,128,128]{2,1,0:T(8,128)} %get-tuple-element.12), custom_call_target="InvertDiagBlocksLowerTriangular" | custom-call | tf_op jit(solution)/shard_map/triangular_solve | solution.py:129
  207.6 1.7 fusion.6
  209.2 1.0 fusion.9
  210.2 1.7 fusion.5
  211.9 1.0 pad_maximum_fusion.1
  213.0 2.5 %copy.63 = f32[1024,256]{1,0:T(8,128)} copy(f32[1024,256]{0,1:T(8,128)} %pad_maximum_fusion.1) | data formatting | bytes 2097152 | tf_op jit(solution)/shard_map/triangular_solve | solution.py:129
  (18 shorter events, 0.3 us)
Async XLA Ops:
  0.0 21.1 %copy-start = (bf16[6,512,512]{2,1,0:T(8,128)(2,1)S(1)}, bf16[6,512,512]{2,1,0:T(8,128)(2,1)}, u32[]{:S(2)}) copy-start(bf16[6,512,512]{2,1,0:T(8,128)(2,1)} %param.5) | copy-start | bytes 9437188
  0.0 13.0 %collective-permute-start = (bf16[1024,256]{1,0:T(8,128)(2,1)}, bf16[1024,256]{1,0:T(8,128)(2,1)S(1)}, u32[]{:S(2)}, u32[]{:S(2)}) collective-permute-start(bf16[1024,256]{1,0:T(8,128)(2,1)} %param.9), channel_id=1, source_target_pairs={{0,1},{1,2},{2,3},{3,4},{4,5},{5,6},{6,7},{7,8},{8,9},{9,10},{10,1... | collective-permute-start | bytes 1572872 | tf_op jit(solution)/shard_map/ppermute | solution.py:20
  4.8 10.7 %collective-permute-start.1 = (bf16[1024,256]{1,0:T(8,128)(2,1)}, bf16[1024,256]{1,0:T(8,128)(2,1)S(1)}, u32[]{:S(2)}, u32[]{:S(2)}) collective-permute-start(bf16[1024,256]{1,0:T(8,128)(2,1)} %param.9), channel_id=1, source_target_pairs={{1,0},{2,1},{3,2},{4,3},{5,4},{6,5},{7,6},{8,7},{9,8},{10,9},{11,1... | collective-permute-start | bytes 1572872 | tf_op jit(solution)/shard_map/ppermute | solution.py:21
  52.8 15.2 %collective-permute-start.2 = (bf16[1024,256]{1,0:T(8,128)(2,1)S(1)}, bf16[1024,256]{1,0:T(8,128)(2,1)S(1)}, u32[]{:S(2)}, u32[]{:S(2)}) collective-permute-start(bf16[1024,256]{1,0:T(8,128)(2,1)S(1)} %bitcast.75), channel_id=1, source_target_pairs={{0,1},{1,2},{2,3},{3,4},{4,5},{5,6},{6,7},{7,8},{8,9},{9,10},{10,1... | collective-permute-start | bytes 1572872 | tf_op jit(solution)/shard_map/ppermute | solution.py:20
  54.8 14.1 %collective-permute-start.3 = (bf16[1024,256]{1,0:T(8,128)(2,1)S(1)}, bf16[1024,256]{1,0:T(8,128)(2,1)S(1)}, u32[]{:S(2)}, u32[]{:S(2)}) collective-permute-start(bf16[1024,256]{1,0:T(8,128)(2,1)S(1)} %bitcast.76), channel_id=1, source_target_pairs={{1,0},{2,1},{3,2},{4,3},{5,4},{6,5},{7,6},{8,7},{9,8},{10,9},{11,1... | collective-permute-start | bytes 1572872 | tf_op jit(solution)/shard_map/ppermute | solution.py:21
  69.1 1.0 copy-start.1
  126.8 12.0 %all-to-all-start.3 = ((bf16[8,64,128]{2,1,0:T(8,128)(2,1)}), bf16[8,64,128]{2,1,0:T(8,128)(2,1)S(1)}, u32[]{:S(2)}, u32[]{:S(2)}) async-start(bf16[8,64,128]{2,1,0:T(8,128)(2,1)} %broadcast_in_dim.37), calls=%async_computation.3 | async-start | bytes 262144 | tf_op jit(solution)/shard_map/all_to_all | solution.py:59
  142.5 0.7 copy-start.3
  178.7 2.1 copy-start.2
where the time goes:
time: 217 us; the launch traced here: 216 us
  other arithmetic  61.5 us (28%)
  blocking collectives  54 us (25%)
  starting transfers between devices  32.2 us (15%)
  local copies, waits for them, and re-layouts  31.6 us (15%)
  matrix products  25.3 us (12%)
  waiting for transfers between devices  8.7 us (4%)
  between operations  2.28 us (1%)
    another operation x6, other arithmetic, on_device(): factor_low = jnp.linalg.cholesky(gram_matrix)  34 us
    another operation x4, other arithmetic, on_device(): lax.linalg.triangular_solve(factor_low, local_y, left_side=False, lower=T...  22.5 us
    all_to_all x1, blocking collectives, summed_on_arrival(): lax.all_to_all(tiles, axis, split_axis=0, concat_axis=0, tiled=True)  20.2 us
    all_to_all x1, blocking collectives, sum_in_two_steps(): lax.all_to_all(own.astype(jnp.bfloat16), far, 0, 0, tiled=True)  19.1 us
    ppermute x2, starting transfers between devices, with_halo(): lax.ppermute(initial, axis, [(b, a) for a, b in up])  18.8 us
    all_to_all x1, blocking collectives, from_everyone(): return lax.all_to_all(copies, axis, split_axis=0, concat_axis=0, tiled=True)  14.7 us
    all_to_all x1, starting transfers between devices, from_everyone(): return lax.all_to_all(copies, axis, split_axis=0, concat_axis=0, tiled=True)  6.72 us
    ppermute x2, starting transfers between devices, with_halo(): lax.ppermute(last, axis, up)  6.67 us
  transfers between devices with their start and end apart: 5, of which 3 were waited for; matrix products, arithmetic and copies ran while one was open for 1% of the time, Pallas kernels for 0%

commit v1 on v0

v1 whole, which is shorter than its diff:
```python
import functools

import jax
import jax.numpy as jnp
from jax import lax
from jax.experimental import pallas as pl
from jax.experimental.pallas import tpu as pltpu
from jax.sharding import Mesh
from jax.sharding import PartitionSpec as P

H = 2
AXES = ("z", "y", "x", "c")
BF16 = jnp.bfloat16
F32 = jnp.float32


def dot(a, b, dims):
    return lax.dot_general(a, b, (dims, ((), ())), preferred_element_type=F32)


NN = ((1,), (0,))
TN = ((0,), (0,))


def step_kernel(
    sizes,
    row_ref, col_ref, count_ref, tiles_hbm, q_hbm,
    y_hbm, gram_ref,
    tiles, q_own, q_left, q_right, aq_acc, aq, rim_low, rim_high, got_left, got_right, y_own,
    terms, rs_in, st_out, s2_in, s3_in, piece,
    load_sem, y_sem, halo_send, halo_recv, rim_send, rim_recv,
    rs_send, rs_recv, s2_send, s2_recv, s3_send, s3_recv, ag_send, ag_recv,
):
    nz, ny, nx, nc = sizes
    bs = tiles.shape[1]
    z, y, x, c = (lax.axis_index(a) for a in AXES)
    me = ((z * ny + y) * nx + x) * nc + c
    total = nz * ny * nx * nc

    def coords(d):
        return (d // (ny * nx * nc), d // (nx * nc) % ny, d // nc % nx, d % nc)

    right, left = coords((me + 1) % total), coords((me + total - 1) % total)
    group = nx * nc
    mine = x * nc + c
    near = []
    for k in range(1, group):
        p = (mine + k) % group
        near.append((p, (z, y, p // nc, p % nc)))
    second = [(z, (y + k) % ny, x, c) for k in range(1, ny)]
    third = [((z + k) % nz, y, x, c) for k in range(1, nz)]
    assert ny == nz
    first_hop, second_hop = [], []
    for k in range(1, ny):
        first_hop.append(((z + k * c) % nz, (y + k * (1 - c)) % ny, x, c))
        second_hop.append(((z + k * (1 - c)) % nz, (y + k * c) % ny, x, c))
    at_first = y * (1 - c) + z * c
    at_second = z * (1 - c) + y * c

    q_load = pltpu.make_async_copy(q_hbm, q_own, load_sem.at[0])
    q_load.start()
    tile_load = pltpu.make_async_copy(tiles_hbm, tiles, load_sem.at[1])
    tile_load.start()

    barrier = pltpu.get_barrier_semaphore()
    peers = [left, right] + [d for _, d in near] + second + third
    for d in peers:
        pl.semaphore_signal(barrier, inc=1, device_id=d, device_id_type=pl.DeviceIdType.MESH)

    slot_count = tiles.shape[0]
    slot, held = {}, {}
    local_row = [row_ref[s] % 2 for s in range(slot_count)]
    offset = [(col_ref[s] - row_ref[s] + H + 2 * total) % (2 * total) for s in range(slot_count)]
    for r in range(2):
        for o in range(2 * H + 1):
            at, live = jnp.int32(0), jnp.int32(0)
            for s in range(slot_count):
                hit = (local_row[s] == r) & (offset[s] == o) & (s < count_ref[0])
                at = jnp.where(hit, s, at)
                live = jnp.where(hit, 1, live)
            slot[r, o], held[r, o] = at, live > 0

    pl.semaphore_wait(barrier, len(peers))
    q_load.wait()

    def send(src, dst, ssem, rsem, device):
        copy = pltpu.make_async_remote_copy(
            src_ref=src, dst_ref=dst, send_sem=ssem, recv_sem=rsem,
            device_id=device, device_id_type=pl.DeviceIdType.MESH,
        )
        copy.start()
        return copy

    to_left = send(q_own, q_right, halo_send.at[0], halo_recv.at[0], left)
    to_right = send(q_own, q_left, halo_send.at[1], halo_recv.at[1], right)
    tile_load.wait()

    def masked(block, r, o):
        return jnp.where(held[r, o], block, jnp.zeros_like(block))

    def forward(r, o, source, at):
        return dot(tiles[slot[r, o]], masked(source[pl.ds(at * bs, bs), :], r, o), NN)

    for r in range(2):
        aq_acc[r] = forward(r, H - r, q_own, 0) + forward(r, H - r + 1, q_own, 1)
    to_right.wait_recv()
    aq_acc[0] = aq_acc[0] + forward(0, 0, q_left, 0) + forward(0, 1, q_left, 1)
    aq_acc[1] = aq_acc[1] + forward(1, 0, q_left, 1)
    to_left.wait_recv()
    aq[0] = (aq_acc[0] + forward(0, 4, q_right, 0)).astype(BF16)
    aq[1] = (aq_acc[1] + forward(1, 3, q_right, 0) + forward(1, 4, q_right, 1)).astype(BF16)

    def backward(r, o):
        return dot(tiles[slot[r, o]], masked(aq[r], r, o), TN)

    low, high = pl.ds(0, bs), pl.ds(bs, bs)
    rim_low[low, :] = backward(0, 0).astype(BF16)
    rim_low[high, :] = (backward(0, 1) + backward(1, 0)).astype(BF16)
    rim_to_left = send(rim_low, got_right, rim_send.at[0], rim_recv.at[0], left)
    rim_high[low, :] = (backward(0, 4) + backward(1, 3)).astype(BF16)
    rim_high[high, :] = backward(1, 4).astype(BF16)
    rim_to_right = send(rim_high, got_left, rim_send.at[1], rim_recv.at[1], right)
    y_own[low, :] = backward(0, 2) + backward(1, 1)
    y_own[high, :] = backward(0, 3) + backward(1, 2)
    rim_to_right.wait_recv()
    rim_to_left.wait_recv()
    whole = y_own[...] + got_left[...].astype(F32) + got_right[...].astype(F32)
    y_own[...] = whole
    y_store = pltpu.make_async_copy(y_own, y_hbm, y_sem)
    y_store.start()
    big = whole.astype(BF16)
    small = (whole - big.astype(F32)).astype(BF16)
    local_gram = dot(big, big, TN) + dot(big, small, TN) + dot(small, big, TN)
    half = local_gram.shape[0] // 2
    rows = 3 * half // group
    terms[0 : half, :] = local_gram[:half, :half].astype(BF16)
    terms[half : 2 * half, :] = local_gram[half:, :half].astype(BF16)
    terms[2 * half :, :] = local_gram[half:, half:].astype(BF16)

    def part(p):
        return pl.ds(pl.multiple_of(p * rows, 16), rows)

    copies = []
    for k, (p, device) in enumerate(near):
        copies.append(
            send(terms.at[part(p), :], rs_in.at[mine], rs_send.at[k], rs_recv.at[k], device)
        )
    rs_in[mine] = terms[part(mine), :]
    for copy in copies:
        copy.wait_recv()
    acc = rs_in[0].astype(F32)
    for p in range(1, group):
        acc = acc + rs_in[p].astype(F32)
    st_out[0] = acc.astype(BF16)
    s2_in[at_first] = acc.astype(BF16)
    hop1 = []
    for k, device in enumerate(first_hop):
        hop1.append(
            send(st_out.at[0], s2_in.at[at_first], s2_send.at[k], s2_recv.at[k], device)
        )
    for copy in hop1:
        copy.wait_recv()
    acc = s2_in[0].astype(F32)
    for p in range(1, ny):
        acc = acc + s2_in[p].astype(F32)
    st_out[1] = acc.astype(BF16)
    s3_in[at_second] = acc.astype(BF16)
    hop2 = []
    for k, device in enumerate(second_hop):
        hop2.append(
            send(st_out.at[1], s3_in.at[at_second], s3_send.at[k], s3_recv.at[k], device)
        )
    for copy in hop2:
        copy.wait_recv()
    acc = s3_in[0].astype(F32)
    for p in range(1, nz):
        acc = acc + s3_in[p].astype(F32)
    piece[...] = acc.astype(BF16)
    gram_ref[part(mine), :] = acc.astype(BF16)
    out = []
    for k, (p, device) in enumerate(near):
        out.append(
            send(piece, gram_ref.at[part(mine), :], ag_send.at[k], ag_recv.at[k], device)
        )
    for copy in out:
        copy.wait_recv()
    y_store.wait()
    for copy in [to_left, to_right, rim_to_left, rim_to_right] + copies + hop1 + hop2 + out:
        copy.wait_send()


def summed_step(sizes, tiles, tile_row, tile_col, tile_count, q_block):
    slots, bs, _ = tiles.shape
    rows, width = q_block.shape
    half = width // 2
    nz, ny, nx, nc = sizes
    group = nx * nc
    part = 3 * half // group
    dma = pltpu.SemaphoreType.DMA
    smem = pl.BlockSpec(memory_space=pltpu.SMEM)
    anywhere = pl.BlockSpec(memory_space=pl.ANY)
    return pl.pallas_call(
        functools.partial(step_kernel, sizes),
        out_shape=(
            jax.ShapeDtypeStruct((rows, width), F32),
            jax.ShapeDtypeStruct((3 * half, half), BF16),
        ),
        in_specs=[smem, smem, smem, anywhere, anywhere],
        out_specs=(anywhere, pl.BlockSpec(memory_space=pltpu.VMEM)),
        scratch_shapes=[
            pltpu.VMEM((slots, bs, bs), BF16),
            pltpu.VMEM((rows, width), BF16),
            pltpu.VMEM((rows, width), BF16),
            pltpu.VMEM((rows, width), BF16),
            pltpu.VMEM((2, bs, width), F32),
            pltpu.VMEM((2, bs, width), BF16),
            pltpu.VMEM((rows, width), BF16),
            pltpu.VMEM((rows, width), BF16),
            pltpu.VMEM((rows, width), BF16),
            pltpu.VMEM((rows, width), BF16),
            pltpu.VMEM((rows, width), F32),
            pltpu.VMEM((3 * half, half), BF16),
            pltpu.VMEM((group, part, half), BF16),
            pltpu.VMEM((2, part, half), BF16),
            pltpu.VMEM((ny, part, half), BF16),
            pltpu.VMEM((nz, part, half), BF16),
            pltpu.VMEM((part, half), BF16),
            dma((2,)), dma, dma((2,)), dma((2,)), dma((2,)), dma((2,)),
            dma((group - 1,)), dma((group - 1,)), dma((ny - 1,)), dma((ny - 1,)),
            dma((nz - 1,)), dma((nz - 1,)), dma((group - 1,)), dma((group - 1,)),
        ],
        compiler_params=pltpu.CompilerParams(
            collective_id=0, has_side_effects=True, vmem_limit_bytes=40 * 1024 * 1024
        ),
        name="step",
    )(tile_row, tile_col, tile_count, tiles, q_block)


def on_device(sizes, tiles, tile_row, tile_col, tile_count, q_block):
    local_y, packed = summed_step(sizes, tiles, tile_row, tile_col, tile_count, q_block)
    half = packed.shape[1]
    blocks = packed.astype(F32)
    corner = blocks[half : 2 * half]
    gram = jnp.concatenate(
        [
            jnp.concatenate([blocks[:half], corner.T], axis=1),
            jnp.concatenate([corner, blocks[2 * half :]], axis=1),
        ],
        axis=0,
    )
    rows_total = local_y.shape[0] * sizes[0] * sizes[1] * sizes[2] * sizes[3]
    factor_low = jnp.linalg.cholesky(gram / rows_total)
    return lax.linalg.triangular_solve(
        factor_low, local_y, left_side=False, lower=True, transpose_a=True
    )


def solution(mesh):
    nz = mesh.shape["grp"]
    sizes = (nz, 8, mesh.shape["row"] // 16, 2)
    torus = Mesh(mesh.devices.reshape(sizes), AXES)
    return jax.shard_map(
        functools.partial(on_device, sizes),
        mesh=torus,
        in_specs=(P(AXES, None, None), P(AXES), P(AXES), P(AXES), P(AXES, None)),
        out_specs=P(AXES, None),
        check_vma=False,
    )
```

time: 217 us -> 125 us (0.58)
  Pallas kernels: 0 us -> 55.7 us
  blocking collectives: 54 us -> 0 us
  starting transfers between devices: 32.2 us -> 0 us
  matrix products: 25.3 us -> 2.7 us
  local copies, waits for them, and re-layouts: 31.6 us -> 9.83 us
  waiting for transfers between devices: 8.7 us -> 0 us
  other arithmetic: 61.5 us -> 54.1 us
    pallas_call x0 -> x1, Pallas kernels: none -> 55.7 us  [summed_step(): pl.pallas_call(functools.partial(step_kernel, sizes), out_shape=(jax.Shap...]
    all_to_all x3 -> x0, blocking collectives: 54 us -> none  [the longest x1 20.2 us: summed_on_arrival(): lax.all_to_all(tiles, axis, split_axis=0, concat_axis=0, tiled=True)]
    ppermute x4 -> x0, starting transfers between devices: 25.4 us -> none  [the longest x2 18.8 us: with_halo(): lax.ppermute(initial, axis, [(b, a) for a, b in up])]
    dot_general x5 -> x0, matrix products: 18.8 us -> none  [the longest x1 4.3 us: on_device(): jnp.einsum('rs,sak->rak', row_place, products, precision=lax.Precision.HI...]
    dot_general x2 -> x0, local copies, waits for them, and re-layouts: 10.2 us -> none  [the longest x1 5.09 us: on_device(): jnp.einsum('sab,sak->sbk', tiles, row_part, preferred_element_type=jnp.fl...]
    all_to_all x1 -> x0, starting transfers between devices: 6.72 us -> none  [from_everyone(): return lax.all_to_all(copies, axis, split_axis=0, concat_axis=0, tiled=True)]
    gather x2 -> x0, local copies, waits for them, and re-layouts: 6.19 us -> none  [the longest x1 3.28 us: on_device(): blocks = stack[local_col]]
    all_to_all x1 -> x0, waiting for transfers between devices: 5.26 us -> none  [from_everyone(): return lax.all_to_all(copies, axis, split_axis=0, concat_axis=0, tiled=True)]
  transfers between devices with their start and end apart: 5 -> 0, of which waited for: 3 -> 0; matrix products, arithmetic and copies ran while one was open for 1% -> 0% of each run, Pallas kernels for 0% -> 0%
where the time goes in v1:
time: 125 us; the launch traced here: 124 us
  Pallas kernels  55.7 us (45%)
  other arithmetic  54.1 us (43%)
  local copies, waits for them, and re-layouts  9.83 us (8%)
  matrix products  2.7 us (2%)
  between operations  2.04 us (2%)
    pallas_call x1, Pallas kernels, summed_step(): pl.pallas_call(functools.partial(step_kernel, sizes), out_shape=(jax.Shap...  55.7 us
    another operation x6, other arithmetic, on_device(): factor_low = jnp.linalg.cholesky(gram / rows_total)  34 us
    another operation x4, other arithmetic, on_device(): lax.linalg.triangular_solve(factor_low, local_y, left_side=False, lower=T...  20 us
    unnamed x9, local copies, waits for them, and re-layouts  4.33 us
    another operation x6, local copies, waits for them, and re-layouts  3.74 us

profile of v1, /device:TPU:1, one launch (start us, length us, event | category | flops | bytes accessed | tf_op | source)
XLA Modules:
  0.0 124.5 jit_solution(12303242421612397060)
XLA Ops:
  0.7 0.1 triangular_solve.58
  0.7 0.0 copy-start
  0.7 1.9 %copy-done = bf16[6,512,512]{2,1,0:T(8,128)(2,1)S(1)} copy-done((bf16[6,512,512]{2,1,0:T(8,128)(2,1)S(1)}, bf16[6,512,512]{2,1,0:T(8,128)(2,1)}, u32[]{:S(2)}) %copy-start) | copy-done | bytes 3145752
  2.6 0.0 copy-start.1
  2.6 1.0 copy-done.1
  3.7 0.0 copy-start.2
  3.7 0.7 copy-done.2
  4.3 0.0 copy-start.3
  4.3 0.7 copy-done.3
  5.0 55.7 %step.1 = (f32[1024,256]{1,0:T(8,128)S(1)}, bf16[384,128]{1,0:T(8,128)(2,1)S(1)}) custom-call(s32[6]{0:T(128)S(1)} %copy-done.2, s32[6]{0:T(128)S(1)} %copy-done.3, s32[1]{0:T(128)S(6)} %copy.22.count_ref, bf16[6,512,512]{2,1,0:T(8,128)(2,1)S(1)} %copy-done, bf16[1024,256]{1,0:T(8,128)(2,1)S(1)} %copy-done.1), custom_call_target="tpu_custom_call" | custom-call | tf_op jit(solution)/shard_map/step/pallas_call | solution.py:202
  60.7 0.1 copy.6
  60.9 0.1 copy.11
  61.0 0.1 copy.8
  61.2 0.1 copy.9
  61.4 11.7 %cholesky.50 = f32[128,128]{1,0:T(8,128)S(1)} custom-call(f32[128,128]{1,0:T(8,128)S(1)} %cholesky.118), custom_call_target="Cholesky" | custom-call | tf_op jit(solution)/shard_map/jit(cholesky)/cholesky | solution.py:252
  73.1 9.8 %custom-call.14 = f32[1,128,128]{1,2,0:T(8,128)S(1)} custom-call(f32[1,128,128]{2,1,0:T(8,128)S(1)} %get-tuple-element.33), custom_call_target="InvertDiagBlocksLowerTriangular" | custom-call | tf_op jit(solution)/shard_map/jit(cholesky)/cholesky | solution.py:252
  82.9 0.2 constant_dynamic-update-slice_fusion.1
  83.2 0.3 convolution_subtract_fusion.1
  83.4 11.7 %cholesky.105 = f32[128,128]{1,0:T(8,128)S(1)} custom-call(f32[128,128]{1,0:T(8,128)S(1)} %convolution_subtract_fusion.1), custom_call_target="Cholesky" | custom-call | tf_op jit(solution)/shard_map/jit(cholesky)/cholesky | solution.py:252
  95.2 0.7 compare_reduce_fusion
  97.1 3.8 %while.1 = (s32[]{:T(128)}, f32[256,256]{1,0:T(8,128)S(1)}, s32[2,2]{1,0:T(2,128)S(1)}, f32[2,128,128]{2,1,0:T(8,128)S(1)}, s32[]{:T(128)}) while((s32[]{:T(128)}, f32[256,256]{1,0:T(8,128)S(1)}, s32[2,2]{1,0:T(2,128)S(1)}, f32[2,128,128]{2,1,0:T(8,128)S(1)}, s32[]{:T(128)}) %tuple.25), condition=%wide.while_cond, body=%wide.while_body.sunk | while | flops 2 | bytes 131189 | solution.py:253
  97.1 0.6 fusion.15
  97.7 1.3 %bitcast_dynamic-update-slice_fusion.2 = f32[2,128,128]{2,1,0:T(8,128)S(1)} fusion(f32[2,128,128]{2,1,0:T(8,128)S(1)} %get-tuple-element.75, s32[]{:T(128)S(6)} %copy.17, f32[256,256]{1,0:T(8,128)S(1)} %get-tuple-element.78, s32[]{:T(128)} %bitcast.31, s32[]{:T(128)} %bitcast.32), kind=kLoop, calls=%fused_computation.clone.1 | loop fusion | bytes 131084 | tf_op jit(solution)/shard_map/triangular_solve
  99.0 0.6 fusion.15
  99.6 1.3 %bitcast_dynamic-update-slice_fusion.2 = f32[2,128,128]{2,1,0:T(8,128)S(1)} fusion(f32[2,128,128]{2,1,0:T(8,128)S(1)} %get-tuple-element.75, s32[]{:T(128)S(6)} %copy.17, f32[256,256]{1,0:T(8,128)S(1)} %get-tuple-element.78, s32[]{:T(128)} %bitcast.31, s32[]{:T(128)} %bitcast.32), kind=kLoop, calls=%fused_computation.clone.1 | loop fusion | bytes 131084 | tf_op jit(solution)/shard_map/triangular_solve
  100.9 19.9 %custom-call.15 = f32[2,128,128]{1,2,0:T(8,128)S(1)} custom-call(f32[2,128,128]{2,1,0:T(8,128)S(1)} %get-tuple-element.16), custom_call_target="InvertDiagBlocksLowerTriangular" | custom-call | tf_op jit(solution)/shard_map/triangular_solve | solution.py:253
  120.8 0.6 fusion
  121.4 1.0 convolution_subtract_fusion
  122.4 0.6 fusion.3
  123.0 0.1 pad_maximum_fusion
  123.1 1.3 %copy.10 = f32[1024,256]{1,0:T(8,128)} copy(f32[1024,256]{0,1:T(8,128)S(1)} %pad_maximum_fusion) | data formatting | bytes 2097152 | tf_op jit(solution)/shard_map/triangular_solve | solution.py:253
  (15 shorter events, 0.3 us)
Async XLA Ops:
  0.7 1.9 %copy-start = (bf16[6,512,512]{2,1,0:T(8,128)(2,1)S(1)}, bf16[6,512,512]{2,1,0:T(8,128)(2,1)}, u32[]{:S(2)}) copy-start(bf16[6,512,512]{2,1,0:T(8,128)(2,1)} %tiles_hbm.1) | copy-start | bytes 9437188
  2.6 1.0 copy-start.1
  3.7 0.7 copy-start.2
  4.3 0.7 copy-start.3

commit v2 on v1

--- a/solution.py
+++ b/solution.py
@@ -20,13 +20,14 @@
 
 NN = ((1,), (0,))
 TN = ((0,), (0,))
+NT = ((1,), (1,))
 
 
 def step_kernel(
     sizes,
     row_ref, col_ref, count_ref, tiles_hbm, q_hbm,
-    y_hbm, gram_ref,
-    tiles, q_own, q_left, q_right, aq_acc, aq, rim_low, rim_high, got_left, got_right, y_own,
+    big_hbm, small_hbm, gram_ref,
+    tiles, q_own, q_left, q_right, aq_acc, aq, rim_low, rim_high, got_left, got_right, y_own, y_big, y_small,
     terms, rs_in, st_out, s2_in, s3_in, piece,
     load_sem, y_sem, halo_send, halo_recv, rim_send, rim_recv,
     rs_send, rs_recv, s2_send, s2_recv, s3_send, s3_recv, ag_send, ag_recv,
@@ -125,17 +126,20 @@
     rim_to_right.wait_recv()
     rim_to_left.wait_recv()
     whole = y_own[...] + got_left[...].astype(F32) + got_right[...].astype(F32)
-    y_own[...] = whole
-    y_store = pltpu.make_async_copy(y_own, y_hbm, y_sem)
-    y_store.start()
     big = whole.astype(BF16)
     small = (whole - big.astype(F32)).astype(BF16)
+    y_big[...] = big
+    y_small[...] = small
     local_gram = dot(big, big, TN) + dot(big, small, TN) + dot(small, big, TN)
     half = local_gram.shape[0] // 2
     rows = 3 * half // group
     terms[0 : half, :] = local_gram[:half, :half].astype(BF16)
     terms[half : 2 * half, :] = local_gram[half:, :half].astype(BF16)
     terms[2 * half :, :] = local_gram[half:, half:].astype(BF16)
+    stores = [
+        pltpu.make_async_copy(y_big, big_hbm, y_sem.at[0]),
+        pltpu.make_async_copy(y_small, small_hbm, y_sem.at[1]),
+    ]
 
     def part(p):
         return pl.ds(pl.multiple_of(p * rows, 16), rows)
@@ -146,6 +150,8 @@
             send(terms.at[part(p), :], rs_in.at[mine], rs_send.at[k], rs_recv.at[k], device)
         )
     rs_in[mine] = terms[part(mine), :]
+    for store in stores:
+        store.start()
     for copy in copies:
         copy.wait_recv()
     acc = rs_in[0].astype(F32)
@@ -184,7 +190,8 @@
         )
     for copy in out:
         copy.wait_recv()
-    y_store.wait()
+    for store in stores:
+        store.wait()
     for copy in [to_left, to_right, rim_to_left, rim_to_right] + copies + hop1 + hop2 + out:
         copy.wait_send()
 
@@ -202,11 +209,12 @@
     return pl.pallas_call(
         functools.partial(step_kernel, sizes),
         out_shape=(
-            jax.ShapeDtypeStruct((rows, width), F32),
+            jax.ShapeDtypeStruct((rows, width), BF16),
+            jax.ShapeDtypeStruct((rows, width), BF16),
             jax.ShapeDtypeStruct((3 * half, half), BF16),
         ),
         in_specs=[smem, smem, smem, anywhere, anywhere],
-        out_specs=(anywhere, pl.BlockSpec(memory_space=pltpu.VMEM)),
+        out_specs=(anywhere, anywhere, pl.BlockSpec(memory_space=pltpu.VMEM)),
         scratch_shapes=[
             pltpu.VMEM((slots, bs, bs), BF16),
             pltpu.VMEM((rows, width), BF16),
@@ -219,13 +227,15 @@
             pltpu.VMEM((rows, width), BF16),
             pltpu.VMEM((rows, width), BF16),
             pltpu.VMEM((rows, width), F32),
+            pltpu.VMEM((rows, width), BF16),
+            pltpu.VMEM((rows, width), BF16),
             pltpu.VMEM((3 * half, half), BF16),
             pltpu.VMEM((group, part, half), BF16),
             pltpu.VMEM((2, part, half), BF16),
             pltpu.VMEM((ny, part, half), BF16),
             pltpu.VMEM((nz, part, half), BF16),
             pltpu.VMEM((part, half), BF16),
-            dma((2,)), dma, dma((2,)), dma((2,)), dma((2,)), dma((2,)),
+            dma((2,)), dma((2,)), dma((2,)), dma((2,)), dma((2,)), dma((2,)),
             dma((group - 1,)), dma((group - 1,)), dma((ny - 1,)), dma((ny - 1,)),
             dma((nz - 1,)), dma((nz - 1,)), dma((group - 1,)), dma((group - 1,)),
         ],
@@ -236,23 +246,134 @@
     )(tile_row, tile_col, tile_count, tiles, q_block)
 
 
+BLOCK = 32
+
+
+def row_of(tile, s):
+    return jnp.broadcast_to(tile[s : s + 1, :], tile.shape)
+
+
+def eliminate(work, inverse, k):
+    n = work.shape[0]
+    start = BLOCK * k
+    tiles, lane_tiles = BLOCK // 8, n // 128
+    own, first = start // 128, start % 128
+    sub = lax.broadcasted_iota(jnp.int32, (8, 128), 0)
+    lane = lax.broadcasted_iota(jnp.int32, (8, 128), 1)
+    inside = (lane >= first) & (lane < first + BLOCK)
+    panel = [
+        [work[start + 8 * i : start + 8 * i + 8, 128 * h : 128 * h + 128] for h in range(lane_tiles)]
+        for i in range(tiles)
+    ]
+    column = {}
+    for j in range(BLOCK):
+        for i in range(j // 8, tiles):
+            diagonal = panel[i][own]
+            column[j, i] = jnp.broadcast_to(diagonal[:, first + j : first + j + 1], (8, 128))
+    for i in range(tiles):
+        unit = jnp.where(lane == sub + (first + 8 * i), 1.0, 0.0)
+        panel[i][own] = jnp.where(inside, unit, panel[i][own])
+    scale = [jnp.zeros((8, 128), F32) for _ in range(tiles)]
+    for j in range(BLOCK):
+        t, s = j // 8, j % 8
+        root = lax.rsqrt(row_of(column[j, t], s))
+        pivot = root * root
+        scale[t] = jnp.where(sub == s, root, scale[t])
+        factor = {i: column[j, i] * pivot for i in range(t, tiles)}
+        factor[t] = jnp.where(sub > s, factor[t], 0.0)
+        for k2 in range(j + 1, BLOCK):
+            value = row_of(column[j, k2 // 8], k2 % 8)
+            for i in range(k2 // 8, tiles):
+                column[k2, i] = column[k2, i] - factor[i] * value
+        for h in range(lane_tiles):
+            value = row_of(panel[t][h], s)
+            for i in range(t, tiles):
+                panel[i][h] = panel[i][h] - factor[i] * value
+    for i in range(tiles):
+        for h in range(lane_tiles):
+            panel[i][h] = panel[i][h] * scale[i]
+            done = lane + 128 * h < start + BLOCK
+            inverse[start + 8 * i : start + 8 * i + 8, 128 * h : 128 * h + 128] = jnp.where(
+                done, panel[i][h], 0.0
+            )
+    rest = start + BLOCK
+    if rest == n:
+        return
+    rows = jnp.concatenate([jnp.concatenate(p, axis=1) for p in panel], axis=0)
+    big = rows.astype(BF16)
+    small = (rows - big.astype(F32)).astype(BF16)
+    base = 128 * (rest // 128)
+    left = jnp.concatenate([big, big, small], axis=0)[:, base:]
+    update = dot(left, jnp.concatenate([big, small, big], axis=0), TN)
+    wide = lax.broadcasted_iota(jnp.int32, (n - rest, n), 1)
+    kept = jnp.where((wide >= start) & (wide < rest), 0.0, work[rest:, :])
+    work[rest:, :] = kept - update[rest - base :, :]
+
+
+def solve_kernel(
+    rows_total, gram_ref, big_hbm, small_hbm, out_hbm,
+    y_big, y_small, work, inverse, out, load_sem, store_sem,
+):
+    loads = [
+        pltpu.make_async_copy(big_hbm, y_big, load_sem.at[0]),
+        pltpu.make_async_copy(small_hbm, y_small, load_sem.at[1]),
+    ]
+    for load in loads:
+        load.start()
+    n = work.shape[0]
+    half = n // 2
+    blocks = gram_ref[...].astype(F32) * (1.0 / rows_total)
+    work[:half, :half] = blocks[:half]
+    work[half:, :half] = blocks[half : 2 * half]
+    work[:half, half:] = blocks[half : 2 * half].T
+    work[half:, half:] = blocks[2 * half :]
+    for k in range(n // BLOCK):
+        eliminate(work, inverse, k)
+    factor = inverse[...]
+    big = factor.astype(BF16)
+    small = (factor - big.astype(F32)).astype(BF16)
+    for load in loads:
+        load.wait()
+    chunk = 256
+    stores = []
+    for i in range(y_big.shape[0] // chunk):
+        span = pl.ds(i * chunk, chunk)
+        out[span, :] = (
+            dot(y_big[span, :], big, NT) + dot(y_big[span, :], small, NT) + dot(y_small[span, :], big, NT)
+        )
+        stores.append(pltpu.make_async_copy(out.at[span, :], out_hbm.at[span, :], store_sem.at[i]))
+        stores[-1].start()
+    for store in stores:
+        store.wait()
+
+
+def solved(rows_total, packed, y_big, y_small):
+    rows, width = y_big.shape
+    anywhere = pl.BlockSpec(memory_space=pl.ANY)
+    dma = pltpu.SemaphoreType.DMA
+    return pl.pallas_call(
+        functools.partial(solve_kernel, rows_total),
+        out_shape=jax.ShapeDtypeStruct((rows, width), F32),
+        in_specs=[pl.BlockSpec(memory_space=pltpu.VMEM), anywhere, anywhere],
+        out_specs=anywhere,
+        scratch_shapes=[
+            pltpu.VMEM((rows, width), BF16),
+            pltpu.VMEM((rows, width), BF16),
+            pltpu.VMEM((width, width), F32),
+            pltpu.VMEM((width, width), F32),
+            pltpu.VMEM((rows, width), F32),
+            dma((2,)),
+            dma((rows // 256,)),
+        ],
+        compiler_params=pltpu.CompilerParams(vmem_limit_bytes=24 * 1024 * 1024),
+        name="solve",
+    )(packed, y_big, y_small)
+
+
 def on_device(sizes, tiles, tile_row, tile_col, tile_count, q_block):
-    local_y, packed = summed_step(sizes, tiles, tile_row, tile_col, tile_count, q_block)
-    half = packed.shape[1]
-    blocks = packed.astype(F32)
-    corner = blocks[half : 2 * half]
-    gram = jnp.concatenate(
-        [
-            jnp.concatenate([blocks[:half], corner.T], axis=1),
-            jnp.concatenate([corner, blocks[2 * half :]], axis=1),
-        ],
-        axis=0,
-    )
-    rows_total = local_y.shape[0] * sizes[0] * sizes[1] * sizes[2] * sizes[3]
-    factor_low = jnp.linalg.cholesky(gram / rows_total)
-    return lax.linalg.triangular_solve(
-        factor_low, local_y, left_side=False, lower=True, transpose_a=True
-    )
+    y_big, y_small, packed = summed_step(sizes, tiles, tile_row, tile_col, tile_count, q_block)
+    rows_total = q_block.shape[0] * sizes[0] * sizes[1] * sizes[2] * sizes[3]
+    return solved(rows_total, packed, y_big, y_small)
 
 
 def solution(mesh):

time: 125 us -> 68.6 us (0.55)
  other arithmetic: 54.1 us -> 0 us
  Pallas kernels: 55.7 us -> 63.5 us
  local copies, waits for them, and re-layouts: 9.83 us -> 4.23 us
  matrix products: 2.7 us -> 0 us
  between operations: 2.04 us -> 0.67 us
    another operation x10 -> x0, other arithmetic: 54 us -> none  [the longest x6 34 us: on_device(): factor_low = jnp.linalg.cholesky(gram / rows_total)]
    pallas_call x0 -> x1, Pallas kernels: none -> 8.06 us  [solved(): pl.pallas_call(functools.partial(solve_kernel, rows_total), out_shape=jax...]
    another operation x10 -> x0, local copies, waits for them, and re-layouts: 5.14 us -> none
    another operation x5 -> x0, matrix products: 2.7 us -> none  [the longest x3 2.23 us: on_device(): lax.linalg.triangular_solve(factor_low, local_y, left_side=False, lower=T...]
    unnamed x9 -> x8, local copies, waits for them, and re-layouts: 4.33 us -> 4.23 us
where the time goes in v2:
time: 68.6 us; the launch traced here: 68.4 us
  Pallas kernels  63.5 us (93%)
  local copies, waits for them, and re-layouts  4.23 us (6%)
    pallas_call x1, Pallas kernels, summed_step(): pl.pallas_call(functools.partial(step_kernel, sizes), out_shape=(jax.Shap...  55.4 us
    pallas_call x1, Pallas kernels, solved(): pl.pallas_call(functools.partial(solve_kernel, rows_total), out_shape=jax...  8.06 us
    unnamed x8, local copies, waits for them, and re-layouts  4.23 us

profile of v2, /device:TPU:1, one launch (start us, length us, event | category | flops | bytes accessed | tf_op | source)
XLA Modules:
  0.0 68.4 jit_solution(5834142746096779045)
XLA Ops:
  0.7 0.0 copy-start
  0.7 1.9 %copy-done = bf16[6,512,512]{2,1,0:T(8,128)(2,1)S(1)} copy-done((bf16[6,512,512]{2,1,0:T(8,128)(2,1)S(1)}, bf16[6,512,512]{2,1,0:T(8,128)(2,1)}, u32[]{:S(2)}) %copy-start) | copy-done | bytes 3145752
  2.5 0.0 copy-start.1
  2.5 1.0 %copy-done.1 = bf16[1024,256]{1,0:T(8,128)(2,1)S(1)} copy-done((bf16[1024,256]{1,0:T(8,128)(2,1)S(1)}, bf16[1024,256]{1,0:T(8,128)(2,1)}, u32[]{:S(2)}) %copy-start.1) | copy-done | bytes 524312
  3.6 0.0 copy-start.2
  3.6 0.7 copy-done.2
  4.2 0.0 copy-start.3
  4.2 0.7 copy-done.3
  4.9 55.4 %step.1 = (bf16[1024,256]{1,0:T(8,128)(2,1)S(1)}, bf16[1024,256]{1,0:T(8,128)(2,1)S(1)}, bf16[384,128]{1,0:T(8,128)(2,1)S(1)}) custom-call(s32[6]{0:T(128)S(1)} %copy-done.2, s32[6]{0:T(128)S(1)} %copy-done.3, s32[1]{0:T(128)S(6)} %copy.6.count_ref, bf16[6,512,512]{2,1,0:T(8,128)(2,1)S(1)} %copy-done, bf16[1024,256]{1,0:T(8,128)(2,1)S(1)} %copy-done.1), custom_call_target="tpu_custom_call" | custom-call | tf_op jit(solution)/shard_map/step/pallas_call | solution.py:209
  60.3 8.1 %solve.1 = f32[1024,256]{1,0:T(8,128)} custom-call(bf16[384,128]{1,0:T(8,128)(2,1)S(1)} %get-tuple-element.8.gram_ref, bf16[1024,256]{1,0:T(8,128)(2,1)S(1)} %get-tuple-element.9.big_hbm, bf16[1024,256]{1,0:T(8,128)(2,1)S(1)} %get-tuple-element.10.small_hbm), custom_call_target="tpu_custom_call" | custom-call | tf_op jit(solution)/shard_map/solve/pallas_call | solution.py:354
Async XLA Ops:
  0.7 1.9 %copy-start = (bf16[6,512,512]{2,1,0:T(8,128)(2,1)S(1)}, bf16[6,512,512]{2,1,0:T(8,128)(2,1)}, u32[]{:S(2)}) copy-start(bf16[6,512,512]{2,1,0:T(8,128)(2,1)} %tiles_hbm.1) | copy-start | bytes 9437188
  2.5 1.0 %copy-start.1 = (bf16[1024,256]{1,0:T(8,128)(2,1)S(1)}, bf16[1024,256]{1,0:T(8,128)(2,1)}, u32[]{:S(2)}) copy-start(bf16[1024,256]{1,0:T(8,128)(2,1)} %q_hbm.1) | copy-start | bytes 1572868
  3.6 0.7 copy-start.2
  4.2 0.7 copy-start.3

commit v3 on v2

--- a/solution.py
+++ b/solution.py
@@ -25,11 +25,11 @@
 
 def step_kernel(
     sizes,
-    row_ref, col_ref, count_ref, tiles_hbm, q_hbm,
-    big_hbm, small_hbm, gram_ref,
-    tiles, q_own, q_left, q_right, aq_acc, aq, rim_low, rim_high, got_left, got_right, y_own, y_big, y_small,
+    count_ref, row_hbm, col_hbm, tiles_hbm, q_hbm,
+    y_big, y_small, gram_ref,
+    row_ref, col_ref, tiles, q_own, q_left, q_right, aq_acc, aq, rim_low, rim_high, got_left, got_right, y_own,
     terms, rs_in, st_out, s2_in, s3_in, piece,
-    load_sem, y_sem, halo_send, halo_recv, rim_send, rim_recv,
+    load_sem, halo_send, halo_recv, rim_send, rim_recv,
     rs_send, rs_recv, s2_send, s2_recv, s3_send, s3_recv, ag_send, ag_recv,
 ):
     nz, ny, nx, nc = sizes
@@ -58,6 +58,10 @@
     at_first = y * (1 - c) + z * c
     at_second = z * (1 - c) + y * c
 
+    index_loads = []
+    for k, (src, dst) in enumerate(((row_hbm, row_ref), (col_hbm, col_ref))):
+        index_loads.append(pltpu.make_async_copy(src, dst, load_sem.at[2 + k]))
+        index_loads[-1].start()
     q_load = pltpu.make_async_copy(q_hbm, q_own, load_sem.at[0])
     q_load.start()
     tile_load = pltpu.make_async_copy(tiles_hbm, tiles, load_sem.at[1])
@@ -68,6 +72,8 @@
     for d in peers:
         pl.semaphore_signal(barrier, inc=1, device_id=d, device_id_type=pl.DeviceIdType.MESH)
 
+    for load in index_loads:
+        load.wait()
     slot_count = tiles.shape[0]
     slot, held = {}, {}
     local_row = [row_ref[s] % 2 for s in range(slot_count)]
@@ -92,8 +98,16 @@
         copy.start()
         return copy
 
-    to_left = send(q_own, q_right, halo_send.at[0], halo_recv.at[0], left)
-    to_right = send(q_own, q_left, halo_send.at[1], halo_recv.at[1], right)
+    to_left, to_right = [], []
+    for k in range(2):
+        tile = pl.ds(k * bs, bs)
+        to_left.append(
+            send(q_own.at[tile], q_right.at[tile], halo_send.at[k], halo_recv.at[k], left)
+        )
+        tile = pl.ds((1 - k) * bs, bs)
+        to_right.append(
+            send(q_own.at[tile], q_left.at[tile], halo_send.at[2 + k], halo_recv.at[2 + k], right)
+        )
     tile_load.wait()
 
     def masked(block, r, o):
@@ -104,42 +118,52 @@
 
     for r in range(2):
         aq_acc[r] = forward(r, H - r, q_own, 0) + forward(r, H - r + 1, q_own, 1)
-    to_right.wait_recv()
-    aq_acc[0] = aq_acc[0] + forward(0, 0, q_left, 0) + forward(0, 1, q_left, 1)
+    to_left[0].wait_recv()
+    aq_acc[0] = aq_acc[0] + forward(0, 4, q_right, 0)
+    aq_acc[1] = aq_acc[1] + forward(1, 3, q_right, 0)
+    to_right[0].wait_recv()
+    aq_acc[0] = aq_acc[0] + forward(0, 1, q_left, 1)
     aq_acc[1] = aq_acc[1] + forward(1, 0, q_left, 1)
-    to_left.wait_recv()
-    aq[0] = (aq_acc[0] + forward(0, 4, q_right, 0)).astype(BF16)
-    aq[1] = (aq_acc[1] + forward(1, 3, q_right, 0) + forward(1, 4, q_right, 1)).astype(BF16)
+    to_right[1].wait_recv()
+    aq[0] = (aq_acc[0] + forward(0, 0, q_left, 0)).astype(BF16)
+    to_left[1].wait_recv()
+    aq[1] = (aq_acc[1] + forward(1, 4, q_right, 1)).astype(BF16)
 
     def backward(r, o):
         return dot(tiles[slot[r, o]], masked(aq[r], r, o), TN)
 
     low, high = pl.ds(0, bs), pl.ds(bs, bs)
+    rim = []
+
+    def send_rim(k, src, dst, span, device):
+        rim.append(send(src.at[span], dst.at[span], rim_send.at[k], rim_recv.at[k], device))
+
     rim_low[low, :] = backward(0, 0).astype(BF16)
+    send_rim(0, rim_low, got_right, low, left)
+    rim_high[low, :] = (backward(0, 4) + backward(1, 3)).astype(BF16)
+    send_rim(1, rim_high, got_left, low, right)
     rim_low[high, :] = (backward(0, 1) + backward(1, 0)).astype(BF16)
-    rim_to_left = send(rim_low, got_right, rim_send.at[0], rim_recv.at[0], left)
-    rim_high[low, :] = (backward(0, 4) + backward(1, 3)).astype(BF16)
+    send_rim(2, rim_low, got_right, high, left)
     rim_high[high, :] = backward(1, 4).astype(BF16)
-    rim_to_right = send(rim_high, got_left, rim_send.at[1], rim_recv.at[1], right)
+    send_rim(3, rim_high, got_left, high, right)
     y_own[low, :] = backward(0, 2) + backward(1, 1)
     y_own[high, :] = backward(0, 3) + backward(1, 2)
-    rim_to_right.wait_recv()
-    rim_to_left.wait_recv()
-    whole = y_own[...] + got_left[...].astype(F32) + got_right[...].astype(F32)
-    big = whole.astype(BF16)
-    small = (whole - big.astype(F32)).astype(BF16)
-    y_big[...] = big
-    y_small[...] = small
-    local_gram = dot(big, big, TN) + dot(big, small, TN) + dot(small, big, TN)
+    grams = []
+    for k, span in enumerate((low, high)):
+        rim[2 * k].wait_recv()
+        rim[2 * k + 1].wait_recv()
+        whole = y_own[span, :] + got_left[span, :].astype(F32) + got_right[span, :].astype(F32)
+        big = whole.astype(BF16)
+        small = (whole - big.astype(F32)).astype(BF16)
+        y_big[span, :] = big
+        y_small[span, :] = small
+        grams.append(dot(big, big, TN) + dot(big, small, TN) + dot(small, big, TN))
+    local_gram = grams[0] + grams[1]
     half = local_gram.shape[0] // 2
     rows = 3 * half // group
     terms[0 : half, :] = local_gram[:half, :half].astype(BF16)
     terms[half : 2 * half, :] = local_gram[half:, :half].astype(BF16)
     terms[2 * half :, :] = local_gram[half:, half:].astype(BF16)
-    stores = [
-        pltpu.make_async_copy(y_big, big_hbm, y_sem.at[0]),
-        pltpu.make_async_copy(y_small, small_hbm, y_sem.at[1]),
-    ]
 
     def part(p):
         return pl.ds(pl.multiple_of(p * rows, 16), rows)
@@ -150,8 +174,6 @@
             send(terms.at[part(p), :], rs_in.at[mine], rs_send.at[k], rs_recv.at[k], device)
         )
     rs_in[mine] = terms[part(mine), :]
-    for store in stores:
-        store.start()
     for copy in copies:
         copy.wait_recv()
     acc = rs_in[0].astype(F32)
@@ -190,9 +212,7 @@
         )
     for copy in out:
         copy.wait_recv()
-    for store in stores:
-        store.wait()
-    for copy in [to_left, to_right, rim_to_left, rim_to_right] + copies + hop1 + hop2 + out:
+    for copy in to_left + to_right + rim + copies + hop1 + hop2 + out:
         copy.wait_send()
 
 
@@ -204,8 +224,8 @@
     group = nx * nc
     part = 3 * half // group
     dma = pltpu.SemaphoreType.DMA
-    smem = pl.BlockSpec(memory_space=pltpu.SMEM)
-    anywhere = pl.BlockSpec(memory_space=pl.ANY)
+    hbm = pl.BlockSpec(memory_space=pltpu.HBM)
+    vmem = pl.BlockSpec(memory_space=pltpu.VMEM)
     return pl.pallas_call(
         functools.partial(step_kernel, sizes),
         out_shape=(
@@ -213,9 +233,11 @@
             jax.ShapeDtypeStruct((rows, width), BF16),
             jax.ShapeDtypeStruct((3 * half, half), BF16),
         ),
-        in_specs=[smem, smem, smem, anywhere, anywhere],
-        out_specs=(anywhere, anywhere, pl.BlockSpec(memory_space=pltpu.VMEM)),
+        in_specs=[pl.BlockSpec(memory_space=pltpu.SMEM)] + [hbm] * 4,
+        out_specs=(vmem, vmem, vmem),
         scratch_shapes=[
+            pltpu.SMEM(tile_row.shape, jnp.int32),
+            pltpu.SMEM(tile_col.shape, jnp.int32),
             pltpu.VMEM((slots, bs, bs), BF16),
             pltpu.VMEM((rows, width), BF16),
             pltpu.VMEM((rows, width), BF16),
@@ -227,15 +249,13 @@
             pltpu.VMEM((rows, width), BF16),
             pltpu.VMEM((rows, width), BF16),
             pltpu.VMEM((rows, width), F32),
-            pltpu.VMEM((rows, width), BF16),
-            pltpu.VMEM((rows, width), BF16),
             pltpu.VMEM((3 * half, half), BF16),
             pltpu.VMEM((group, part, half), BF16),
             pltpu.VMEM((2, part, half), BF16),
             pltpu.VMEM((ny, part, half), BF16),
             pltpu.VMEM((nz, part, half), BF16),
             pltpu.VMEM((part, half), BF16),
-            dma((2,)), dma((2,)), dma((2,)), dma((2,)), dma((2,)), dma((2,)),
+            dma((4,)), dma((4,)), dma((4,)), dma((4,)), dma((4,)),
             dma((group - 1,)), dma((group - 1,)), dma((ny - 1,)), dma((ny - 1,)),
             dma((nz - 1,)), dma((nz - 1,)), dma((group - 1,)), dma((group - 1,)),
         ],
@@ -243,7 +263,13 @@
             collective_id=0, has_side_effects=True, vmem_limit_bytes=40 * 1024 * 1024
         ),
         name="step",
-    )(tile_row, tile_col, tile_count, tiles, q_block)
+    )(
+        tile_count,
+        *(
+            pltpu.with_memory_space_constraint(a, pltpu.HBM)
+            for a in (tile_row, tile_col, tiles, q_block)
+        ),
+    )
 
 
 BLOCK = 32
@@ -311,15 +337,8 @@
 
 
 def solve_kernel(
-    rows_total, gram_ref, big_hbm, small_hbm, out_hbm,
-    y_big, y_small, work, inverse, out, load_sem, store_sem,
+    rows_total, gram_ref, y_big, y_small, out_hbm, work, inverse, out, store_sem,
 ):
-    loads = [
-        pltpu.make_async_copy(big_hbm, y_big, load_sem.at[0]),
-        pltpu.make_async_copy(small_hbm, y_small, load_sem.at[1]),
-    ]
-    for load in loads:
-        load.start()
     n = work.shape[0]
     half = n // 2
     blocks = gram_ref[...].astype(F32) * (1.0 / rows_total)
@@ -332,8 +351,6 @@
     factor = inverse[...]
     big = factor.astype(BF16)
     small = (factor - big.astype(F32)).astype(BF16)
-    for load in loads:
-        load.wait()
     chunk = 256
     stores = []
     for i in range(y_big.shape[0] // chunk):
@@ -349,21 +366,17 @@
 
 def solved(rows_total, packed, y_big, y_small):
     rows, width = y_big.shape
-    anywhere = pl.BlockSpec(memory_space=pl.ANY)
-    dma = pltpu.SemaphoreType.DMA
+    vmem = pl.BlockSpec(memory_space=pltpu.VMEM)
     return pl.pallas_call(
         functools.partial(solve_kernel, rows_total),
         out_shape=jax.ShapeDtypeStruct((rows, width), F32),
-        in_specs=[pl.BlockSpec(memory_space=pltpu.VMEM), anywhere, anywhere],
-        out_specs=anywhere,
+        in_specs=[vmem, vmem, vmem],
+        out_specs=pl.BlockSpec(memory_space=pltpu.HBM),
         scratch_shapes=[
-            pltpu.VMEM((rows, width), BF16),
-            pltpu.VMEM((rows, width), BF16),
             pltpu.VMEM((width, width), F32),
             pltpu.VMEM((width, width), F32),
             pltpu.VMEM((rows, width), F32),
-            dma((2,)),
-            dma((rows // 256,)),
+            pltpu.SemaphoreType.DMA((rows // 256,)),
         ],
         compiler_params=pltpu.CompilerParams(vmem_limit_bytes=24 * 1024 * 1024),
         name="solve",

time: 68.6 us -> 62.2 us (0.907)
  local copies, waits for them, and re-layouts: 4.23 us -> 0 us
  Pallas kernels: 63.5 us -> 61.4 us
    unnamed x8 -> x0, local copies, waits for them, and re-layouts: 4.23 us -> none
    pallas_call x1, Pallas kernels: 55.4 us -> 53.6 us  [summed_step(): pl.pallas_call(functools.partial(step_kernel, sizes), out_shape=(jax.Shap...]
where the time goes in v3:
time: 62.2 us; the launch traced here: 62 us
  Pallas kernels  61.4 us (99%)
  between operations  0.66 us (1%)
    pallas_call x1, Pallas kernels, summed_step(): pl.pallas_call(functools.partial(step_kernel, sizes), out_shape=(jax.Shap...  53.6 us
    pallas_call x1, Pallas kernels, solved(): pl.pallas_call(functools.partial(solve_kernel, rows_total), out_shape=jax...  7.75 us

profile of v3, /device:TPU:1, one launch (start us, length us, event | category | flops | bytes accessed | tf_op | source)
XLA Modules:
  0.0 62.0 jit_solution(9576049105481865125)
XLA Ops:
  0.7 53.6 %step.1 = (bf16[1024,256]{1,0:T(8,128)(2,1)S(1)}, bf16[1024,256]{1,0:T(8,128)(2,1)S(1)}, bf16[384,128]{1,0:T(8,128)(2,1)S(1)}) custom-call(s32[1]{0:T(128)S(6)} %copy.6.count_ref, s32[6]{0:T(128)} %row_hbm.1, s32[6]{0:T(128)} %col_hbm.1, bf16[6,512,512]{2,1,0:T(8,128)(2,1)} %tiles_hbm.1, bf16[1024,256]{1,0:T(8,128)(2,1)} %q_hbm.1), custom_call_target="tpu_custom_call" | custom-call | tf_op jit(solution)/shard_map/step/pallas_call | solution.py:229
  54.3 7.7 %solve.1 = f32[1024,256]{1,0:T(8,128)} custom-call(bf16[384,128]{1,0:T(8,128)(2,1)S(1)} %get-tuple-element.8.gram_ref, bf16[1024,256]{1,0:T(8,128)(2,1)S(1)} %get-tuple-element.9.y_big, bf16[1024,256]{1,0:T(8,128)(2,1)S(1)} %get-tuple-element.10.y_small), custom_call_target="tpu_custom_call" | custom-call | tf_op jit(solution)/shard_map/solve/pallas_call | solution.py:370
